TPU v7x, 32 devices: a whole 2x2x4 slice. The times are simulated.
32 devices in a mesh: seq: 8 (over z, y), tp: 4 (over x, core).
Axes of the slice: x: 2, y: 2, z: 4, core: 2. Of those that a mesh axis runs over, the one named last changes fastest.
Arguments:
- tokens: bfloat16 [4096, 2048], P('seq'), may hold values from -16 to 16
- forget: float32 [4096, 32], P('seq', 'tp'), may hold values from -5 to 0, as said below
- attn_gain: float32 [2048], replicated, may hold values from 0.1 to 1.9
- projections: bfloat16 [3, 2048, 2048], P(None, None, 'tp'), may hold values from -0.125 to 0.125
- out_weight: bfloat16 [2048, 2048], P('tp'), may hold values from -0.125 to 0.125
- ffn_gain: float32 [2048], replicated, may hold values from 0.1 to 1.9
- expand_weight: bfloat16 [2, 2048, 4096], P(None, None, 'tp'), may hold values from -0.125 to 0.125
- down_weight: bfloat16 [4096, 2048], P('tp'), may hold values from -0.09375 to 0.09375
Outputs:
- output: bfloat16 [4096, 2048], P('seq')
Inputs may be any that keep to these rules, and one draw needn't show every extreme that they name: forget is never positive.
All inputs are finite; a program needn't handle non-finite values.
Results may differ from a plain program's by a relative error of at most 0.011.
Values may be sent and summed in bfloat16 or wider, within the bound.
A program may use at most 128 MiB of HBM per device.

v0:
```python
import functools

import jax
import jax.numpy as jnp
from jax import lax
from jax.experimental import pallas as pl
from jax.experimental.pallas import tpu as pltpu
from jax.sharding import PartitionSpec as P

norm_epsilon = 1e-05
head_epsilon = 1e-06
MESH = pl.DeviceIdType.MESH
CHUNKS = 4
F32 = jnp.float32
BF16 = jnp.bfloat16


def dot(a, b):
    return jnp.dot(a, b, preferred_element_type=F32)


def contract(a, b, dim_a, dim_b):
    return lax.dot_general(
        a, b, (((dim_a,), (dim_b,)), ((), ())), preferred_element_type=F32
    )


def normalize(widened, gain):
    mean_square = jnp.mean(widened * widened, axis=-1, keepdims=True)
    return (widened * lax.rsqrt(mean_square + norm_epsilon) * gain).astype(BF16)


def kernel(
    blocks, steps,
    tok_hbm, fgt, again, proj_hbm, ow_hbm, fgain, ew_hbm, dw_hbm,
    out_hbm,
    tok, wq, wk, wv, wo, wg, wu, wd,
    normed, q, k, v, att, ho, bd, es, el, ts, tl, tsb, tsl, trb, trl,
    part, own, dsend1, drecv1, xsend1, xrecv1, nf, res, hid,
    dsend2, drecv2, xsend2, xrecv2, outb,
    ld, ldt,
    wsem, sts, strv, d1s, d1r, x1s, x1r, ns, nr, d2s, d2r, x2s, x2r, osd, orv, olc,
):
    rows, width = tok.shape
    heads = fgt.shape[0]
    pairs = heads // 2
    chunk = rows // CHUNKS
    half = chunk // 2
    me = lax.axis_index("seq")
    tp = lax.axis_index("tp")
    core = lax.rem(tp, 2)
    partner = tp + 1 - 2 * core
    across = lax.rem(tp + 2, 4)

    loads = []
    for at, (src, dst) in enumerate((
        (tok_hbm, tok), (proj_hbm.at[1], wk), (proj_hbm.at[2], wv), (proj_hbm.at[0], wq),
        (ow_hbm, wo), (ew_hbm.at[0], wg), (ew_hbm.at[1], wu), (dw_hbm, wd),
    )):
        copy = pltpu.make_async_copy(src, dst, wsem.at[at])
        loads.append(copy)
    for at in range(3):
        loads[at].start()

    barrier = pltpu.get_barrier_semaphore()
    for other in (partner, across):
        pl.semaphore_signal(barrier, inc=1, device_id={"tp": other}, device_id_type=MESH)
    for step in range(steps):
        for far in (2 ** step, blocks - 2 ** step):
            pl.semaphore_signal(
                barrier, inc=1, device_id={"seq": lax.rem(me + far, blocks)}, device_id_type=MESH)

    tri = (
        lax.broadcasted_iota(jnp.int32, (rows, rows), 0)
        >= lax.broadcasted_iota(jnp.int32, (rows, rows), 1)
    ).astype(F32)
    ld[...] = lax.dot_general(
        tri, fgt[...], (((1,), (1,)), ((), ())),
        precision=lax.Precision.HIGHEST, preferred_element_type=F32,
    )
    ldt[...] = lax.dot_general(
        fgt[...], tri, (((1,), (1,)), ((), ())),
        precision=lax.Precision.HIGHEST, preferred_element_type=F32,
    )

    loads[0].wait()
    loads[3].start()
    loads[4].start()

    def norm_chunk(r, carry):
        at = pl.ds(pl.multiple_of(r * chunk, chunk), chunk)
        normed[at, :] = normalize(tok[at, :].astype(F32), again[...])
        return carry

    lax.fori_loop(0, CHUNKS, norm_chunk, 0)

    def project(weight, dst):
        tile = min(256, dst.shape[1])

        def body(j, carry):
            at = pl.ds(pl.multiple_of(j * tile, tile), tile)
            dst[:, at] = dot(normed[...], weight[:, at]).astype(BF16)
            return carry

        lax.fori_loop(0, dst.shape[1] // tile, body, 0)

    loads[1].wait()
    project(wk, k)
    loads[2].wait()
    project(wv, v)

    low = lax.broadcasted_iota(jnp.int32, (1, 128), 1) < 64
    low_f = low.astype(F32)
    masks_f = (low_f, 1.0 - low_f)
    masks = (masks_f[0].astype(BF16), masks_f[1].astype(BF16))

    def spread(columns, p):
        return jnp.where(low, columns[:, 2 * p : 2 * p + 1], columns[:, 2 * p + 1 : 2 * p + 2])

    log_decay = ld[...]
    last = log_decay[rows - 1 : rows, :]
    shrink = jnp.exp(last - log_decay)
    tl[...] = jnp.zeros_like(tl)
    el[...] = jnp.zeros_like(el)
    es[...] = jnp.zeros_like(es)
    for p in range(pairs):
        lanes = slice(128 * p, 128 * p + 128)
        scaled = (k[:, lanes].astype(F32) * spread(shrink, p)).astype(BF16)
        state = contract(scaled, v[:, lanes], 0, 0)
        ts[64 * p : 64 * p + 64, :] = state[:64] * masks_f[0] + state[64:] * masks_f[1]
        tl[p : p + 1, :] = spread(last, p)

    pl.semaphore_wait(barrier, 2 + 2 * steps)

    def state_copies(step):
        far = 2 ** step
        return (
            pltpu.make_async_remote_copy(
                tsb.at[step], trb.at[step], sts.at[step, 0], strv.at[step, 0],
                device_id={"seq": me + far}, device_id_type=MESH),
            pltpu.make_async_remote_copy(
                tsl.at[step], trl.at[step], sts.at[step, 1], strv.at[step, 1],
                device_id={"seq": me + far}, device_id_type=MESH),
        )

    def send_state(step):
        @pl.when(me + 2 ** step < blocks)
        def _():
            tsb[step] = ts[...].astype(BF16)
            tsl[step] = tl[...]
            for copy in state_copies(step):
                copy.start()

    def take_state(step):
        @pl.when(me >= 2 ** step)
        def _():
            for copy in state_copies(step):
                copy.wait_recv()
            e_decay = jnp.exp(el[...])
            t_decay = jnp.exp(tl[...])
            for p in range(pairs):
                at = slice(64 * p, 64 * p + 64)
                came = trb[step, at, :].astype(F32)
                es[at, :] = es[at, :] + e_decay[p : p + 1, :] * came
                ts[at, :] = ts[at, :] + t_decay[p : p + 1, :] * came
            el[...] = el[...] + trl[step]
            tl[...] = tl[...] + trl[step]

        if step + 1 < steps:
            send_state(step + 1)

    if steps:
        send_state(0)
    for at in (5, 6, 7):
        loads[at].start()
    loads[3].wait()
    project(wq, q)

    span = rows // 2
    taken = 0
    for p in range(pairs):
        lanes = slice(128 * p, 128 * p + 128)
        for piece in range(2):
            at = slice(piece * span, piece * span + span)
            reach = (piece + 1) * span
            causal = (
                lax.broadcasted_iota(jnp.int32, (span, reach), 0) + piece * span
                >= lax.broadcasted_iota(jnp.int32, (span, reach), 1)
            )
            sums = []
            for j in range(2):
                h = 2 * p + j
                scores = contract(q[at, lanes] * masks[j], k[:reach, lanes], 1, 1)
                gaps = jnp.where(causal, ld[at, h : h + 1] - ldt[h : h + 1, :reach], -1e30)
                weights = (scores * 0.125 * jnp.exp(gaps)).astype(BF16)
                sums.append(dot(weights, v[:reach, lanes]))
            att[at, lanes] = jnp.where(low, sums[0], sums[1])
        if p % 2 and taken < steps:
            take_state(taken)
            taken += 1
    while taken < steps:
        take_state(taken)
        taken += 1

    for p in range(pairs):
        came = es[64 * p : 64 * p + 64, :]
        bd[p] = jnp.concatenate([came * masks_f[0], came * masks_f[1]], axis=0).astype(BF16)
    same_head = (
        (lax.broadcasted_iota(jnp.int32, (128, 128), 0) < 64)
        == (lax.broadcasted_iota(jnp.int32, (128, 128), 1) < 64)
    ).astype(F32).astype(BF16)

    def whole_rows(r):
        return pl.ds(pl.multiple_of(r * chunk, chunk), chunk)

    def own_rows(r):
        return pl.ds(pl.multiple_of(r * chunk + core * half, half), half)

    mine = pl.ds(pl.multiple_of(core * half, half), half)
    theirs = pl.ds(pl.multiple_of(half - core * half, half), half)

    def to(src, dst, ssem, rsem, other):
        return pltpu.make_async_remote_copy(
            src, dst, ssem, rsem, device_id={"tp": other}, device_id_type=MESH)

    def d1(r):
        return to(dsend1.at[r], drecv1.at[r], d1s.at[r], d1r.at[r], partner)

    def x1(r):
        return to(xsend1.at[r], xrecv1.at[r], x1s.at[r], x1r.at[r], across)

    def nfc(r):
        return to(nf.at[own_rows(r)], nf.at[own_rows(r)], ns.at[r], nr.at[r], partner)

    def d2(r):
        return to(dsend2.at[r], drecv2.at[r], d2s.at[r], d2r.at[r], partner)

    def x2(r):
        return to(xsend2.at[r], xrecv2.at[r], x2s.at[r], x2r.at[r], across)

    def oc(r):
        return to(outb.at[r], out_hbm.at[own_rows(r)], osd.at[r], orv.at[r], partner)

    def ol(r):
        return pltpu.make_async_copy(outb.at[r], out_hbm.at[own_rows(r)], olc.at[r])

    loads[4].wait()
    wide = min(512, width)

    def attend(r, carry):
        at = whole_rows(r)
        reach_decay = jnp.exp(ld[at, :]) * 0.125
        for p in range(pairs):
            lanes = slice(128 * p, 128 * p + 128)
            attended = att[at, lanes] + dot(q[at, lanes], bd[p]) * spread(reach_decay, p)
            mean_square = dot((attended * attended).astype(BF16), same_head) * (1.0 / 64)
            ho[at, lanes] = (attended * lax.rsqrt(mean_square + head_epsilon)).astype(BF16)
        for c in range(width // wide):
            cols = slice(c * wide, c * wide + wide)
            part[:, cols] = dot(ho[at, :], wo[:, cols])
        own[r] = part[mine, :]
        dsend1[r] = part[theirs, :].astype(BF16)
        d1(r).start()
        return carry

    def cross1(r):
        d1(r).wait_recv()
        xsend1[r] = (own[r] + drecv1[r].astype(F32)).astype(BF16)
        x1(r).start()

    def attend_cross(r, carry):
        attend(r, 0)

        @pl.when(r > 0)
        def _():
            cross1(r - 1)

        return carry

    lax.fori_loop(0, CHUNKS, attend_cross, 0)
    cross1(CHUNKS - 1)
    for at in (5, 6, 7):
        loads[at].wait()

    hidden_width = wg.shape[1]
    tile = min(256, hidden_width)

    def forward(r, carry):
        x1(r).wait_recv()
        added = xsend1[r].astype(F32) + xrecv1[r].astype(F32)
        kept = (tok[own_rows(r), :].astype(F32) + added).astype(BF16)
        res[r] = kept
        nf[own_rows(r), :] = normalize(kept.astype(F32), fgain[...])
        nfc(r).start()
        nfc(r).wait_recv()
        at = whole_rows(r)
        for c in range(hidden_width // tile):
            cols = slice(c * tile, c * tile + tile)
            gate = dot(nf[at, :], wg[:, cols])
            up = dot(nf[at, :], wu[:, cols])
            hid[:, cols] = (gate / (1.0 + jnp.exp(-gate)) * up).astype(BF16)
        for c in range(width // wide):
            cols = slice(c * wide, c * wide + wide)
            part[:, cols] = dot(hid[...], wd[:, cols])
        own[r] = part[mine, :]
        dsend2[r] = part[theirs, :].astype(BF16)
        d2(r).start()
        d2(r).wait_recv()
        xsend2[r] = (own[r] + drecv2[r].astype(F32)).astype(BF16)
        x2(r).start()
        return carry

    lax.fori_loop(0, CHUNKS, forward, 0)

    def finish(r, carry):
        x2(r).wait_recv()
        added = xsend2[r].astype(F32) + xrecv2[r].astype(F32)
        outb[r] = (res[r].astype(F32) + added).astype(BF16)
        oc(r).start()
        ol(r).start()
        return carry

    lax.fori_loop(0, CHUNKS, finish, 0)

    def drain(r, carry):
        for copy in (d1(r), x1(r), nfc(r), d2(r), x2(r)):
            copy.wait_send()
        oc(r).wait()
        ol(r).wait()
        return carry

    lax.fori_loop(0, CHUNKS, drain, 0)
    for step in range(steps):
        @pl.when(me + 2 ** step < blocks)
        def _():
            for copy in state_copies(step):
                copy.wait_send()


def local(blocks, tokens, forget, attn_gain, projections, out_weight, ffn_gain, expand_weight, down_weight):
    rows, width = tokens.shape
    heads = forget.shape[1]
    inner = projections.shape[2]
    hidden = down_weight.shape[0]
    pairs = heads // 2
    steps = max(blocks - 1, 0).bit_length()
    chunk = rows // CHUNKS
    half = chunk // 2
    V = pltpu.VMEM
    S = pltpu.SemaphoreType.DMA
    slots = max(steps, 1)
    piece = V((CHUNKS, half, width), BF16)
    scratch = [
        V((rows, width), BF16),
        V((width, inner), BF16), V((width, inner), BF16), V((width, inner), BF16),
        V((inner, width), BF16),
        V((width, hidden), BF16), V((width, hidden), BF16), V((hidden, width), BF16),
        V((rows, width), BF16),
        V((rows, inner), BF16), V((rows, inner), BF16), V((rows, inner), BF16),
        V((rows, inner), F32), V((rows, inner), BF16),
        V((pairs, 128, 128), BF16),
        V((64 * pairs, 128), F32), V((8, 128), F32), V((64 * pairs, 128), F32), V((8, 128), F32),
        V((slots, 64 * pairs, 128), BF16), V((slots, 8, 128), F32),
        V((slots, 64 * pairs, 128), BF16), V((slots, 8, 128), F32),
        V((chunk, width), F32), V((CHUNKS, half, width), F32),
        piece, piece, piece, piece,
        V((rows, width), BF16), piece, V((chunk, hidden), BF16),
        piece, piece, piece, piece, piece,
        V((rows, heads), F32), V((heads, rows), F32),
        S((8,)), S((slots, 2)), S((slots, 2)),
    ] + [S((CHUNKS,)) for _ in range(13)]
    hbm = pl.BlockSpec(memory_space=pl.ANY)
    vmem = pl.BlockSpec(memory_space=pltpu.VMEM)
    return pl.pallas_call(
        functools.partial(kernel, blocks, steps),
        out_shape=jax.ShapeDtypeStruct((rows, width), BF16),
        in_specs=[hbm, vmem, vmem, hbm, hbm, vmem, hbm, hbm],
        out_specs=hbm,
        scratch_shapes=scratch,
        compiler_params=pltpu.CompilerParams(
            collective_id=0, has_side_effects=True, vmem_limit_bytes=64_000_000
        ),
    )(
        tokens, forget.T, attn_gain[None, :], projections, out_weight,
        ffn_gain[None, :], expand_weight, down_weight,
    )


def solution(mesh):
    placed = (
        P("seq", None),
        P("seq", "tp"),
        P(),
        P(None, None, "tp"),
        P("tp", None),
        P(),
        P(None, None, "tp"),
        P("tp", None),
    )
    return jax.shard_map(
        functools.partial(local, mesh.shape["seq"]),
        mesh=mesh, in_specs=placed, out_specs=P("seq", None), check_vma=False,
    )
```

profile of v0, /device:TPU:25, one launch (start us, length us, event | category | flops | bytes accessed | tf_op | source)
XLA Modules:
  0.0 71.8 jit_solution(7447334791919478524)
XLA Ops:
  0.0 68.7 %shard_map.82 = bf16[512,2048]{1,0:T(8,128)(2,1)} custom-call(bf16[512,2048]{1,0:T(8,128)(2,1)} %tok_hbm.1, f32[8,512]{1,0:T(8,128)} %bitcast.3, f32[1,2048]{1,0:T(1,128)} %bitcast.4, bf16[3,2048,512]{2,1,0:T(8,128)(2,1)} %proj_hbm.1, bf16[512,2048]{1,0:T(8,128)(2,1)} %ow_hbm.1, f32[1,2048]{1,0:T(1,128)} %bitcast.5, bf16[2,2048,1024]{2,1,0:T(8,128)(2,1)} %ew_hbm.1, ...), custom_call_target="tpu_custom_call" | custom-call | tf_op jit(solution)/shard_map/pallas_call | solution.py:374
  68.7 3.2 %copy.10 = bf16[512,2048]{1,0:T(8,128)(2,1)} copy(bf16[512,2048]{1,0:T(8,128)(2,1)} %shard_map.82) | data formatting | bytes 4194304
where the time goes:
time: 72.1 us; the launch traced here: 71.8 us
  Pallas kernels  68.7 us (95%)
  local copies, waits for them, and re-layouts  3.16 us (4%)
    pallas_call x1, Pallas kernels, local(): pl.pallas_call(functools.partial(kernel, blocks, steps), out_shape=jax.Sh...  68.7 us
    unnamed x1, local copies, waits for them, and re-layouts  3.16 us

commit v1 on v0

v1 whole, which is shorter than its diff:
```python
import functools

import jax
import jax.numpy as jnp
from jax import lax
from jax.experimental import pallas as pl
from jax.experimental.pallas import tpu as pltpu
from jax.sharding import PartitionSpec as P

norm_epsilon = 1e-05
head_epsilon = 1e-06
MESH = pl.DeviceIdType.MESH
CHUNKS = 4
SIZES = (2, 2, 2, 2)
PLAIN = 1
SUB = 8
VIA_Z = ()
VIA_Y = (0, 1, 2, 3, 4)
STRAIGHT = (5, 6, 7)
F32 = jnp.float32
BF16 = jnp.bfloat16


def dot(a, b):
    return jnp.dot(a, b, preferred_element_type=F32)


def contract(a, b, dim_a, dim_b):
    return lax.dot_general(
        a, b, (((dim_a,), (dim_b,)), ((), ())), preferred_element_type=F32
    )


def normalize(widened, gain):
    mean_square = jnp.mean(widened * widened, axis=-1, keepdims=True)
    return (widened * lax.rsqrt(mean_square + norm_epsilon) * gain).astype(BF16)


def kernel(
    blocks, steps,
    tok_hbm, fgt, again, proj_hbm, ow_hbm, fgain, ew_hbm, dw_hbm,
    out,
    tok, wq, wk, wv, wo, wg, wu, wd,
    normed, q, k, v, att, ho, bd, es, el, ts, tl, ed, td, tsb, tsl, trb, trl,
    part, own, dsend1, drecv1, xsend1, xrecv1, nf, res, hid,
    dsend2, drecv2, xsend2, xrecv2,
    ks, ld, ldt,
    wsem, tsem, sts, strv, wxs, wxr, wys, wyr, wzs, wzr, wcs, wcr,
    d1s, d1r, x1s, x1r, hs, hr, ns, nr, d2s, d2r, x2s, x2r, osd, orv,
):
    rows, width = tok.shape
    heads = fgt.shape[0]
    inner = wk.shape[1]
    pairs = heads // 2
    chunk = rows // CHUNKS
    me = lax.axis_index("seq")
    tp = lax.axis_index("tp")
    core = lax.rem(tp, 2)
    side = lax.div(tp, 2)
    partner = tp + 1 - 2 * core
    across = lax.rem(tp + 2, 4)
    place = lax.rem(me, 4)
    bit_y = lax.rem(me, 2)
    bit_z = lax.div(place, 2)
    next_y = me + 1 - 2 * bit_y
    next_z = me + 2 - 4 * bit_z

    loads = []
    for at, (src, dst) in enumerate((
        (proj_hbm.at[1], wk), (proj_hbm.at[2], wv), (proj_hbm.at[0], wq),
        (ow_hbm, wo.at[side]), (ew_hbm.at[0], wg), (ew_hbm.at[1], wu), (dw_hbm, wd),
    )):
        copy = pltpu.make_async_copy(src, dst, wsem.at[at])
        loads.append(copy)
    def token_load(r):
        at = pl.ds(pl.multiple_of(r * chunk, chunk), chunk)
        return pltpu.make_async_copy(tok_hbm.at[at], tok.at[at], tsem.at[r])

    for r in range(CHUNKS):
        token_load(r).start()

    barrier = pltpu.get_barrier_semaphore()
    for other in (partner, across):
        pl.semaphore_signal(barrier, inc=1, device_id={"tp": other}, device_id_type=MESH)
    for other in (next_y, next_z):
        pl.semaphore_signal(barrier, inc=1, device_id={"seq": other}, device_id_type=MESH)
    for step in range(1, steps):
        for far in (2 ** step, blocks - 2 ** step):
            pl.semaphore_signal(
                barrier, inc=1, device_id={"seq": lax.rem(me + far, blocks)}, device_id_type=MESH)

    quarter = inner // 4
    sub = quarter // SUB

    def strip(owner, j):
        return pl.ds(pl.multiple_of(owner * quarter + j * sub, sub), sub)

    def on_seq(src, dst, ssem, rsem, other):
        return pltpu.make_async_remote_copy(
            src, dst, ssem, rsem, device_id={"seq": other}, device_id_type=MESH)

    def to(src, dst, ssem, rsem, other):
        return pltpu.make_async_remote_copy(
            src, dst, ssem, rsem, device_id={"tp": other}, device_id_type=MESH)

    far_wo = wo.at[1 - side]
    place_y = place + 1 - 2 * bit_y
    place_z = place + 2 - 4 * bit_z

    def wx(j):
        return to(ow_hbm.at[strip(place, j)], wo.at[side, strip(place, j)], wxs.at[j], wxr.at[j], across)

    def wy(j):
        at = strip(place, j)
        return on_seq(far_wo.at[at], far_wo.at[at], wys.at[j], wyr.at[j], next_y)

    def wz(j):
        at = strip(place, j)
        return on_seq(far_wo.at[at], far_wo.at[at], wzs.at[j], wzr.at[j], next_z)

    def wc(j):
        at = strip(3 - place, j)
        return to(ow_hbm.at[at], wo.at[side, at], wcs.at[j], wcr.at[j], across)

    def corner(j):
        if j in VIA_Z:
            at = strip(place_y, j)
            return on_seq(far_wo.at[at], far_wo.at[at], wcs.at[j], wcr.at[j], next_z)
        at = strip(place_z, j)
        return on_seq(far_wo.at[at], far_wo.at[at], wcs.at[j], wcr.at[j], next_y)

    def pass_y(j):
        wx(j).wait_recv()
        wy(j).start()

    def pass_z(j):
        wz(j).start()

    def pass_corner(j):
        if j in VIA_Z:
            wy(j).wait_recv()
        else:
            wz(j).wait_recv()
        corner(j).start()

    runs = rows // 128
    tri = (
        lax.broadcasted_iota(jnp.int32, (128, 128), 0)
        <= lax.broadcasted_iota(jnp.int32, (128, 128), 1)
    ).astype(F32).astype(BF16)
    rounded = []
    for b in range(runs):
        left = fgt[:, 128 * b : 128 * b + 128]
        for _ in range(3):
            top = left.astype(BF16).astype(F32)
            rounded.append(top)
            left = left - top
    sums = dot(jnp.concatenate(rounded, axis=0).astype(BF16), tri)
    carried = jnp.zeros((heads, 1), F32)
    for b in range(runs):
        at = 3 * heads * b
        run = sums[at : at + heads] + sums[at + heads : at + 2 * heads]
        run = run + sums[at + 2 * heads : at + 3 * heads] + carried
        ldt[:, 128 * b : 128 * b + 128] = run
        ld[128 * b : 128 * b + 128, :] = run.T
        carried = run[:, 127:128]
    loads[0].start()
    pl.semaphore_wait(barrier, 4 + 2 * (steps - 1))
    for j in range(SUB):
        wx(j).start()
    for j in STRAIGHT:
        wc(j).start()


    def norm_chunk(r, carry):
        at = pl.ds(pl.multiple_of(r * chunk, chunk), chunk)
        token_load(r).wait()
        normed[at, :] = normalize(tok[at, :].astype(F32), again[...])
        return carry

    loads[1].start()
    lax.fori_loop(0, CHUNKS, norm_chunk, 0)

    def project(weight, dst):
        tile = min(256, dst.shape[1])

        def body(j, carry):
            at = pl.ds(pl.multiple_of(j * tile, tile), tile)
            dst[:, at] = dot(normed[...], weight[:, at]).astype(BF16)
            return carry

        lax.fori_loop(0, dst.shape[1] // tile, body, 0)

    loads[2].start()
    loads[3].start()
    loads[0].wait()
    project(wk, k)
    loads[1].wait()

    low = lax.broadcasted_iota(jnp.int32, (1, 128), 1) < 64
    low_f = low.astype(F32)
    masks_f = (low_f, 1.0 - low_f)
    masks = (masks_f[0].astype(BF16), masks_f[1].astype(BF16))

    def spread(columns, p):
        return jnp.where(low, columns[:, 2 * p : 2 * p + 1], columns[:, 2 * p + 1 : 2 * p + 2])

    log_decay = ld[...]
    last = log_decay[rows - 1 : rows, :]
    shrink = jnp.exp(ldt[:, rows - 1 : rows] - ldt[...])
    tl[...] = jnp.zeros_like(tl)
    el[...] = jnp.zeros_like(el)
    es[...] = jnp.zeros_like(es)
    for p in range(pairs):
        tl[p : p + 1, :] = spread(last, p)
    part_pairs = pairs // 2

    later = bit_y == 1

    def heir(step):
        return me + 2 ** step if step else next_y

    def sends(step):
        return me + 2 ** step < blocks if step else me >= 0

    def takes(step):
        return me >= 2 ** step if step else me >= 0

    def state_copy(step, part_of):
        at = slice(64 * part_pairs * part_of, 64 * part_pairs * (part_of + 1))
        return pltpu.make_async_remote_copy(
            tsb.at[step, at], trb.at[step, at], sts.at[step, part_of], strv.at[step, part_of],
            device_id={"seq": heir(step)}, device_id_type=MESH)

    def decay_copy(step):
        return pltpu.make_async_remote_copy(
            tsl.at[step], trl.at[step], sts.at[step, 2], strv.at[step, 2],
            device_id={"seq": heir(step)}, device_id_type=MESH)

    def state_copies(step):
        return (decay_copy(step), state_copy(step, 0), state_copy(step, 1))

    def send_state(step, part_of):
        @pl.when(sends(step))
        def _():
            at = slice(64 * part_pairs * part_of, 64 * part_pairs * (part_of + 1))
            if part_of == 0:
                tsl[step] = tl[...]
                decay_copy(step).start()
            tsb[step, at, :] = ts[at, :].astype(BF16)
            state_copy(step, part_of).start()

    def take_state(step):
        for part_of in range(2):
            @pl.when(takes(step))
            def _():
                if part_of == 0:
                    decay_copy(step).wait_recv()
                    ed[...] = jnp.exp(el[...])
                    td[...] = jnp.exp(tl[...])
                    if step == 0:
                        td[...] = jnp.where(later, td[...], jnp.exp(trl[step]))
                        el[...] = jnp.where(later, trl[step], el[...])
                    else:
                        el[...] = el[...] + trl[step]
                    tl[...] = tl[...] + trl[step]
                state_copy(step, part_of).wait_recv()
                for p in range(part_pairs * part_of, part_pairs * (part_of + 1)):
                    at = slice(64 * p, 64 * p + 64)
                    came = trb[step, at, :].astype(F32)
                    decay = td[p : p + 1, :]
                    if step == 0:
                        mine_first = ts[at, :]
                        es[at, :] = jnp.where(later, came, 0.0)
                        ts[at, :] = jnp.where(
                            later, mine_first + decay * came, decay * mine_first + came)
                    else:
                        es[at, :] = es[at, :] + ed[p : p + 1, :] * came
                        ts[at, :] = ts[at, :] + decay * came

            if step + 1 < steps:
                send_state(step + 1, part_of)

    for p in range(pairs):
        turned = k[:, 128 * p : 128 * p + 128].T.astype(F32)
        for j in range(2):
            h = 2 * p + j
            ks[64 * h : 64 * h + 64, :] = (turned[64 * j : 64 * j + 64] * shrink[h : h + 1, :]).astype(BF16)
    each = 128 * part_pairs
    for part_of in range(2):
        cols = slice(each * part_of, each * (part_of + 1))
        v[:, cols] = dot(normed[...], wv[:, cols]).astype(BF16)
        state = dot(ks[cols, :], v[:, cols])
        for p in range(part_pairs):
            at = slice(128 * p, 128 * p + 128)
            pair = state[at, at]
            h = 64 * (part_pairs * part_of + p)
            ts[h : h + 64, :] = pair[:64] * masks_f[0] + pair[64:] * masks_f[1]
        if steps:
            send_state(0, part_of)

    for at in (4, 5, 6):
        loads[at].start()
    loads[2].wait()
    project(wq, q)

    span = rows // 2
    taken = 0
    for p in range(pairs):
        lanes = slice(128 * p, 128 * p + 128)
        for piece in range(2):
            at = slice(piece * span, piece * span + span)
            reach = (piece + 1) * span
            causal = (
                lax.broadcasted_iota(jnp.int32, (span, reach), 0) + piece * span
                >= lax.broadcasted_iota(jnp.int32, (span, reach), 1)
            )
            sums = []
            for j in range(2):
                h = 2 * p + j
                scores = contract(q[at, lanes] * masks[j], k[:reach, lanes], 1, 1)
                gaps = jnp.where(causal, ld[at, h : h + 1] - ldt[h : h + 1, :reach], -1e30)
                weights = (scores * 0.125 * jnp.exp(gaps)).astype(BF16)
                sums.append(dot(weights, v[:reach, lanes]))
            att[at, lanes] = jnp.where(low, sums[0], sums[1])
            if p % 2 == 0 and piece and taken < steps:
                take_state(taken)
                taken += 1
                if taken == 1:
                    for j in range(3):
                        pass_y(j)
        if p == pairs - 2:
            pass_y(3)
    for j in (4, 5):
        pass_y(j)
    while taken < steps:
        take_state(taken)
        taken += 1

    for j in range(6, SUB):
        pass_y(j)
    for j in range(SUB):
        pass_z(j)

    for p in range(pairs):
        came = es[64 * p : 64 * p + 64, :]
        bd[p] = jnp.concatenate([came * masks_f[0], came * masks_f[1]], axis=0).astype(BF16)
    same_head = (
        (lax.broadcasted_iota(jnp.int32, (128, 128), 0) < 64)
        == (lax.broadcasted_iota(jnp.int32, (128, 128), 1) < 64)
    ).astype(F32).astype(BF16)

    starts, total = [], 0
    for size in SIZES:
        starts.append(total * (rows // sum(SIZES)))
        total += size
    sizes = [size * (rows // sum(SIZES)) for size in SIZES]
    count = len(sizes)

    def whole_rows(r):
        return slice(starts[r], starts[r] + sizes[r])

    def half_rows(r):
        return slice(starts[r] // 2, starts[r] // 2 + sizes[r] // 2)

    def own_rows(r):
        half = sizes[r] // 2
        return pl.ds(pl.multiple_of(starts[r] + core * half, half), half)

    def mine(r):
        half = sizes[r] // 2
        return pl.ds(pl.multiple_of(core * half, half), half)

    def theirs(r):
        half = sizes[r] // 2
        return pl.ds(pl.multiple_of(half - core * half, half), half)

    def d1(r):
        at = half_rows(r)
        return to(dsend1.at[at], drecv1.at[at], d1s.at[r], d1r.at[r], partner)

    def x1(r):
        at = half_rows(r)
        return to(xsend1.at[at], xrecv1.at[at], x1s.at[r], x1r.at[r], across)

    def hx(r):
        at = whole_rows(r)
        return to(ho.at[side, at], ho.at[side, at], hs.at[r], hr.at[r], across)

    def nfc(r):
        return to(nf.at[own_rows(r)], nf.at[own_rows(r)], ns.at[r], nr.at[r], partner)

    def d2(r):
        at = half_rows(r)
        return to(dsend2.at[at], drecv2.at[at], d2s.at[r], d2r.at[r], partner)

    def x2(r, piece):
        n = sizes[r] // 4
        at = pl.ds(starts[r] // 2 + piece * n, n)
        return to(xsend2.at[at], xrecv2.at[at], x2s.at[r, piece], x2r.at[r, piece], across)

    def oc(r, piece):
        at = out_rows(r, piece)
        return to(out.at[at], out.at[at], osd.at[r, piece], orv.at[r, piece], partner)

    def out_rows(r, piece):
        n = sizes[r] // 4
        return pl.ds(pl.multiple_of(starts[r] + core * 2 * n + piece * n, n), n)

    loads[3].wait()
    wide = min(512, width)

    def attend(r):
        at = whole_rows(r)
        reach_decay = jnp.exp(ld[at, :]) * 0.125
        for p in range(pairs):
            lanes = slice(128 * p, 128 * p + 128)
            attended = att[at, lanes] + dot(q[at, lanes], bd[p]) * spread(reach_decay, p)
            mean_square = dot((attended * attended).astype(BF16), same_head) * (1.0 / 64)
            ho[side, at, lanes] = (attended * lax.rsqrt(mean_square + head_epsilon)).astype(BF16)

    def halve(r, send, copy):
        n = sizes[r]
        own[half_rows(r), :] = part[mine(r), :]
        send[half_rows(r), :] = part[theirs(r), :].astype(BF16)
        copy.start()

    def combine(r):
        at, n = whole_rows(r), sizes[r]
        for c in range(width // wide):
            cols = slice(c * wide, c * wide + wide)
            if r < PLAIN:
                part[:n, cols] = dot(ho[side, at, :], wo[side, :, cols])
            else:
                part[:n, cols] = dot(ho[0, at, :], wo[0, :, cols]) + dot(ho[1, at, :], wo[1, :, cols])
        halve(r, dsend1, d1(r))

    def cross(r):
        at = half_rows(r)
        d1(r).wait_recv()
        xsend1[at, :] = (own[at, :] + drecv1[at, :].astype(F32)).astype(BF16)
        x1(r).start()

    def settle(r):
        at = half_rows(r)
        if r < PLAIN:
            x1(r).wait_recv()
            added = xsend1[at, :].astype(F32) + xrecv1[at, :].astype(F32)
        else:
            d1(r).wait_recv()
            added = own[at, :] + drecv1[at, :].astype(F32)
        kept = (tok[own_rows(r), :].astype(F32) + added).astype(BF16)
        res[at, :] = kept
        nf[own_rows(r), :] = normalize(kept.astype(F32), fgain[...])
        nfc(r).start()

    hidden_width = wg.shape[1]
    tile = min(256, hidden_width)

    def forward(r):
        nfc(r).wait_recv()
        at, n = whole_rows(r), sizes[r]
        for c in range(hidden_width // tile):
            cols = slice(c * tile, c * tile + tile)
            gate = dot(nf[at, :], wg[:, cols])
            up = dot(nf[at, :], wu[:, cols])
            hid[:n, cols] = (gate / (1.0 + jnp.exp(-gate)) * up).astype(BF16)
        for c in range(width // wide):
            cols = slice(c * wide, c * wide + wide)
            part[:n, cols] = dot(hid[:n, :], wd[:, cols])
        halve(r, dsend2, d2(r))

    def pass_sums(r):
        at = half_rows(r)
        d2(r).wait_recv()
        xsend2[at, :] = (own[at, :] + drecv2[at, :].astype(F32)).astype(BF16)
        x2(r, 0).start()
        x2(r, 1).start()

    def finish(r, piece):
        n = sizes[r] // 4
        at = slice(starts[r] // 2 + piece * n, starts[r] // 2 + piece * n + n)
        x2(r, piece).wait_recv()
        added = xsend2[at, :].astype(F32) + xrecv2[at, :].astype(F32)
        out[out_rows(r, piece), :] = (res[at, :].astype(F32) + added).astype(BF16)
        oc(r, piece).start()

    if PLAIN < count:
        attend(PLAIN)
        hx(PLAIN).start()
    for r in range(PLAIN):
        attend(r)
        combine(r)
    for r in range(PLAIN + 1, count):
        attend(r)
    for r in range(PLAIN):
        cross(r)
    for r in range(PLAIN + 1, count):
        hx(r).start()
    for at in (4, 5, 6):
        loads[at].wait()

    def arrive():
        for j in range(SUB):
            if j not in VIA_Z:
                wy(j).wait_recv()
            if j not in VIA_Y:
                wz(j).wait_recv()
            if j in STRAIGHT:
                wc(j).wait_recv()
            else:
                corner(j).wait_recv()

    def combine_late(r):
        if r == PLAIN:
            arrive()
        hx(r).wait_recv()
        combine(r)

    for j in VIA_Z + VIA_Y:
        pass_corner(j)
    settle(0)
    for r in range(count):
        if PLAIN < r + 1 < count:
            combine_late(r + 1)
        if r > PLAIN:
            pass_sums(r - 1)
        forward(r)
        if r + 1 == PLAIN < count:
            combine_late(r + 1)
        if r < PLAIN:
            pass_sums(r)
        if r + 1 < count:
            settle(r + 1)
    pass_sums(count - 1)
    for j in range(SUB):
        for copy in (wx(j), wy(j), wz(j), wc(j) if j in STRAIGHT else corner(j)):
            copy.wait_send()
    for step in range(steps):
        @pl.when(sends(step))
        def _():
            for copy in state_copies(step):
                copy.wait_send()
    for r in range(count):
        for copy in (d1(r), nfc(r), d2(r), x1(r) if r < PLAIN else hx(r)):
            copy.wait_send()
    for r in range(count):
        for piece in range(2):
            finish(r, piece)
    for r in range(count):
        for piece in range(2):
            x2(r, piece).wait_send()
            oc(r, piece).wait()


def local(blocks, tokens, forget, attn_gain, projections, out_weight, ffn_gain, expand_weight, down_weight):
    rows, width = tokens.shape
    heads = forget.shape[1]
    inner = projections.shape[2]
    hidden = down_weight.shape[0]
    pairs = heads // 2
    steps = max(blocks - 1, 0).bit_length()
    V = pltpu.VMEM
    S = pltpu.SemaphoreType.DMA
    slots = max(steps, 1)
    count = len(SIZES)
    largest = rows // sum(SIZES) * max(SIZES)
    halves = V((rows // 2, width), BF16)
    early = V((rows // sum(SIZES) * sum(SIZES[:max(PLAIN, 1)]) // 2, width), BF16)
    scratch = [
        V((rows, width), BF16),
        V((width, inner), BF16), V((width, inner), BF16), V((width, inner), BF16),
        V((2, inner, width), BF16),
        V((width, hidden), BF16), V((width, hidden), BF16), V((hidden, width), BF16),
        V((rows, width), BF16),
        V((rows, inner), BF16), V((rows, inner), BF16), V((rows, inner), BF16),
        V((rows, inner), F32), V((2, rows, inner), BF16),
        V((pairs, 128, 128), BF16),
        V((64 * pairs, 128), F32), V((8, 128), F32), V((64 * pairs, 128), F32), V((8, 128), F32),
        V((8, 128), F32), V((8, 128), F32),
        V((slots, 64 * pairs, 128), BF16), V((slots, 8, 128), F32),
        V((slots, 64 * pairs, 128), BF16), V((slots, 8, 128), F32),
        V((largest, width), F32), V((rows // 2, width), F32),
        halves, halves, early, early,
        V((rows, width), BF16), halves, V((largest, hidden), BF16),
        halves, halves, halves, halves,
        V((inner, rows), BF16), V((rows, heads), F32), V((heads, rows), F32),
        S((8,)), S((CHUNKS,)), S((slots, 3)), S((slots, 3)),
    ] + [S((SUB,)) for _ in range(8)] + [S((count,)) for _ in range(10)] + [S((count, 2)) for _ in range(4)]
    hbm = pl.BlockSpec(memory_space=pl.ANY)
    vmem = pl.BlockSpec(memory_space=pltpu.VMEM)
    return pl.pallas_call(
        functools.partial(kernel, blocks, steps),
        out_shape=pltpu.VMEM((rows, width), BF16),
        in_specs=[hbm, vmem, vmem, hbm, hbm, vmem, hbm, hbm],
        out_specs=vmem,
        scratch_shapes=scratch,
        compiler_params=pltpu.CompilerParams(
            collective_id=0, has_side_effects=True, vmem_limit_bytes=60_000_000
        ),
    )(
        tokens, forget.T, attn_gain[None, :], projections, out_weight,
        ffn_gain[None, :], expand_weight, down_weight,
    )


def solution(mesh):
    placed = (
        P("seq", None),
        P("seq", "tp"),
        P(),
        P(None, None, "tp"),
        P("tp", None),
        P(),
        P(None, None, "tp"),
        P("tp", None),
    )
    return jax.shard_map(
        functools.partial(local, mesh.shape["seq"]),
        mesh=mesh, in_specs=placed, out_specs=P("seq", None), check_vma=False,
    )
```

time: 72.1 us -> 65.7 us (0.911)
  the two profiles are of different devices: /device:TPU:25 before, /device:TPU:0 now
where the time goes in v1:
time: 65.7 us; the launch traced here: 65.5 us
  Pallas kernels  64.1 us (98%)
  local copies, waits for them, and re-layouts  1.32 us (2%)
    pallas_call x1, Pallas kernels, local(): pl.pallas_call(functools.partial(kernel, blocks, steps), out_shape=pltpu....  64.1 us
    unnamed x1, local copies, waits for them, and re-layouts  1.32 us

profile of v1, /device:TPU:0, one launch (start us, length us, event | category | flops | bytes accessed | tf_op | source)
XLA Modules:
  0.0 65.5 jit_solution(9845446665118024230)
XLA Ops:
  0.0 64.1 %shard_map.82 = bf16[512,2048]{1,0:T(8,128)(2,1)S(1)} custom-call(bf16[512,2048]{1,0:T(8,128)(2,1)} %tok_hbm.1, f32[8,512]{1,0:T(8,128)} %bitcast.3, f32[1,2048]{1,0:T(1,128)} %bitcast.4, bf16[3,2048,512]{2,1,0:T(8,128)(2,1)} %proj_hbm.1, bf16[512,2048]{1,0:T(8,128)(2,1)} %ow_hbm.1, f32[1,2048]{1,0:T(1,128)} %bitcast.5, bf16[2,2048,1024]{2,1,0:T(8,128)(2,1)} %ew_hbm.1, ...), custom_call_target="tpu_custom_call" | custom-call | tf_op jit(solution)/shard_map/pallas_call | solution.py:592
  64.1 1.3 %copy.10 = bf16[512,2048]{1,0:T(8,128)(2,1)} copy(bf16[512,2048]{1,0:T(8,128)(2,1)S(1)} %shard_map.82) | data formatting | bytes 4194304

commit v2 on v1

--- a/solution.py
+++ b/solution.py
@@ -14,9 +14,9 @@
 SIZES = (2, 2, 2, 2)
 PLAIN = 1
 SUB = 8
-VIA_Z = ()
-VIA_Y = (0, 1, 2, 3, 4)
-STRAIGHT = (5, 6, 7)
+VIA_Z = (0,)
+VIA_Y = (1, 2, 3, 4, 5)
+STRAIGHT = (6, 7)
 F32 = jnp.float32
 BF16 = jnp.bfloat16
 
@@ -38,14 +38,15 @@
 
 def kernel(
     blocks, steps,
-    tok_hbm, fgt, again, proj_hbm, ow_hbm, fgain, ew_hbm, dw_hbm,
+    tok_hbm, fgt_hbm, again_hbm, proj_hbm, ow_hbm, fgain_hbm, ew_hbm, dw_hbm,
     out,
+    fgt, again, fgain,
     tok, wq, wk, wv, wo, wg, wu, wd,
     normed, q, k, v, att, ho, bd, es, el, ts, tl, ed, td, tsb, tsl, trb, trl,
     part, own, dsend1, drecv1, xsend1, xrecv1, nf, res, hid,
     dsend2, drecv2, xsend2, xrecv2,
     ks, ld, ldt,
-    wsem, tsem, sts, strv, wxs, wxr, wys, wyr, wzs, wzr, wcs, wcr,
+    wsem, tsem, small_sem, sts, strv, wxs, wxr, wys, wyr, wzs, wzr, wcs, wcr,
     d1s, d1r, x1s, x1r, hs, hr, ns, nr, d2s, d2r, x2s, x2r, osd, orv,
 ):
     rows, width = tok.shape
@@ -76,18 +77,29 @@
         at = pl.ds(pl.multiple_of(r * chunk, chunk), chunk)
         return pltpu.make_async_copy(tok_hbm.at[at], tok.at[at], tsem.at[r])
 
+    small = []
+    for at, (src, dst) in enumerate(((fgt_hbm, fgt), (again_hbm, again), (fgain_hbm, fgain))):
+        small.append(pltpu.make_async_copy(src, dst, small_sem.at[at]))
+    small[0].start()
     for r in range(CHUNKS):
         token_load(r).start()
+    small[1].start()
+    small[2].start()
 
     barrier = pltpu.get_barrier_semaphore()
     for other in (partner, across):
         pl.semaphore_signal(barrier, inc=1, device_id={"tp": other}, device_id_type=MESH)
     for other in (next_y, next_z):
         pl.semaphore_signal(barrier, inc=1, device_id={"seq": other}, device_id_type=MESH)
+    greeted = 4
     for step in range(1, steps):
-        for far in (2 ** step, blocks - 2 ** step):
-            pl.semaphore_signal(
-                barrier, inc=1, device_id={"seq": lax.rem(me + far, blocks)}, device_id_type=MESH)
+        far = 2 ** step
+        for reached, other in ((me + far < blocks, me + far), (me >= far, me - far)):
+            greeted = greeted + reached.astype(jnp.int32)
+
+            @pl.when(reached)
+            def _():
+                pl.semaphore_signal(barrier, inc=1, device_id={"seq": other}, device_id_type=MESH)
 
     quarter = inner // 4
     sub = quarter // SUB
@@ -129,12 +141,20 @@
         at = strip(place_z, j)
         return on_seq(far_wo.at[at], far_wo.at[at], wcs.at[j], wcr.at[j], next_y)
 
-    def pass_y(j):
-        wx(j).wait_recv()
-        wy(j).start()
-
-    def pass_z(j):
-        wz(j).start()
+    far_half = me >= blocks // 2
+
+    def pass_pieces(cond, pieces):
+        @pl.when(cond)
+        def _():
+            for name, j in pieces:
+                if "w" in name:
+                    wx(j).wait_recv()
+                if "y" in name:
+                    wy(j).start()
+                if "z" in name:
+                    wz(j).start()
+
+    near = jnp.logical_not(far_half)
 
     def pass_corner(j):
         if j in VIA_Z:
@@ -148,6 +168,7 @@
         lax.broadcasted_iota(jnp.int32, (128, 128), 0)
         <= lax.broadcasted_iota(jnp.int32, (128, 128), 1)
     ).astype(F32).astype(BF16)
+    small[0].wait()
     rounded = []
     for b in range(runs):
         left = fgt[:, 128 * b : 128 * b + 128]
@@ -165,12 +186,15 @@
         ld[128 * b : 128 * b + 128, :] = run.T
         carried = run[:, 127:128]
     loads[0].start()
-    pl.semaphore_wait(barrier, 4 + 2 * (steps - 1))
-    for j in range(SUB):
-        wx(j).start()
-    for j in STRAIGHT:
-        wc(j).start()
-
+
+    def enter():
+        pl.semaphore_wait(barrier, greeted)
+        for j in range(SUB):
+            wx(j).start()
+        for j in STRAIGHT:
+            wc(j).start()
+
+    pl.when(me >= blocks // 2)(enter)
 
     def norm_chunk(r, carry):
         at = pl.ds(pl.multiple_of(r * chunk, chunk), chunk)
@@ -179,6 +203,8 @@
         return carry
 
     loads[1].start()
+    small[1].wait()
+    small[2].wait()
     lax.fori_loop(0, CHUNKS, norm_chunk, 0)
 
     def project(weight, dst):
@@ -194,7 +220,10 @@
     loads[2].start()
     loads[3].start()
     loads[0].wait()
-    project(wk, k)
+    for c in range(2):
+        cols = slice(c * (inner // 2), (c + 1) * (inner // 2))
+        k[:, cols] = dot(normed[...], wk[:, cols]).astype(BF16)
+    pl.when(near)(enter)
     loads[1].wait()
 
     low = lax.broadcasted_iota(jnp.int32, (1, 128), 1) < 64
@@ -296,12 +325,12 @@
             pair = state[at, at]
             h = 64 * (part_pairs * part_of + p)
             ts[h : h + 64, :] = pair[:64] * masks_f[0] + pair[64:] * masks_f[1]
-        if steps:
-            send_state(0, part_of)
+        send_state(0, part_of)
 
     for at in (4, 5, 6):
         loads[at].start()
     loads[2].wait()
+    pass_pieces(far_half, (("wz", 0), ("wz", 1)))
     project(wq, q)
 
     span = rows // 2
@@ -327,20 +356,20 @@
                 take_state(taken)
                 taken += 1
                 if taken == 1:
-                    for j in range(3):
-                        pass_y(j)
-        if p == pairs - 2:
-            pass_y(3)
-    for j in (4, 5):
-        pass_y(j)
+                    pass_pieces(far_half, (("y", 0), ("y", 1), ("wy", 2)))
+                elif taken == 2:
+                    pass_pieces(far_half, (("wy", 4),))
+                    pass_pieces(near, (("wyz", 0),))
+        if p == 1:
+            pass_pieces(far_half, (("wy", 3),))
+        if p == pairs - 1:
+            pass_pieces(far_half, (("wy", 5),))
+            pass_pieces(near, (("wyz", 1),))
     while taken < steps:
         take_state(taken)
         taken += 1
 
-    for j in range(6, SUB):
-        pass_y(j)
-    for j in range(SUB):
-        pass_z(j)
+    pass_pieces(far_half, [("z", j) for j in range(2, 6)] + [("wyz", 6)])
 
     for p in range(pairs):
         came = es[64 * p : 64 * p + 64, :]
@@ -491,12 +520,15 @@
     for r in range(PLAIN):
         attend(r)
         combine(r)
+    pass_pieces(far_half, (("wyz", 7),))
+    pass_pieces(near, (("wyz", 2), ("wyz", 3)))
     for r in range(PLAIN + 1, count):
         attend(r)
     for r in range(PLAIN):
         cross(r)
     for r in range(PLAIN + 1, count):
         hx(r).start()
+    pass_pieces(near, [("wyz", j) for j in range(4, SUB)])
     for at in (4, 5, 6):
         loads[at].wait()
 
@@ -568,6 +600,7 @@
     halves = V((rows // 2, width), BF16)
     early = V((rows // sum(SIZES) * sum(SIZES[:max(PLAIN, 1)]) // 2, width), BF16)
     scratch = [
+        V((heads, rows), F32), V((1, width), F32), V((1, width), F32),
         V((rows, width), BF16),
         V((width, inner), BF16), V((width, inner), BF16), V((width, inner), BF16),
         V((2, inner, width), BF16),
@@ -585,14 +618,14 @@
         V((rows, width), BF16), halves, V((largest, hidden), BF16),
         halves, halves, halves, halves,
         V((inner, rows), BF16), V((rows, heads), F32), V((heads, rows), F32),
-        S((8,)), S((CHUNKS,)), S((slots, 3)), S((slots, 3)),
+        S((8,)), S((CHUNKS,)), S((3,)), S((slots, 3)), S((slots, 3)),
     ] + [S((SUB,)) for _ in range(8)] + [S((count,)) for _ in range(10)] + [S((count, 2)) for _ in range(4)]
     hbm = pl.BlockSpec(memory_space=pl.ANY)
     vmem = pl.BlockSpec(memory_space=pltpu.VMEM)
     return pl.pallas_call(
         functools.partial(kernel, blocks, steps),
         out_shape=pltpu.VMEM((rows, width), BF16),
-        in_specs=[hbm, vmem, vmem, hbm, hbm, vmem, hbm, hbm],
+        in_specs=[hbm] * 8,
         out_specs=vmem,
         scratch_shapes=scratch,
         compiler_params=pltpu.CompilerParams(

time: 65.7 us -> 63.4 us (0.965)
  Pallas kernels: 64.1 us -> 62 us
    pallas_call x1, Pallas kernels: 64.1 us -> 62 us  [local(): pl.pallas_call(functools.partial(kernel, blocks, steps), out_shape=pltpu....]
where the time goes in v2:
time: 63.4 us; the launch traced here: 63.3 us
  Pallas kernels  62 us (98%)
  local copies, waits for them, and re-layouts  1.32 us (2%)
    pallas_call x1, Pallas kernels, local(): pl.pallas_call(functools.partial(kernel, blocks, steps), out_shape=pltpu....  62 us
    unnamed x1, local copies, waits for them, and re-layouts  1.32 us

profile of v2, /device:TPU:0, one launch (start us, length us, event | category | flops | bytes accessed | tf_op | source)
XLA Modules:
  0.0 63.3 jit_solution(18395993833502436410)
XLA Ops:
  0.0 62.0 %shard_map.82 = bf16[512,2048]{1,0:T(8,128)(2,1)S(1)} custom-call(bf16[512,2048]{1,0:T(8,128)(2,1)} %tok_hbm.1, f32[8,512]{1,0:T(8,128)} %bitcast.3, f32[1,2048]{1,0:T(1,128)} %bitcast.4, bf16[3,2048,512]{2,1,0:T(8,128)(2,1)} %proj_hbm.1, bf16[512,2048]{1,0:T(8,128)(2,1)} %ow_hbm.1, f32[1,2048]{1,0:T(1,128)} %bitcast.5, bf16[2,2048,1024]{2,1,0:T(8,128)(2,1)} %ew_hbm.1, ...), custom_call_target="tpu_custom_call" | custom-call | tf_op jit(solution)/shard_map/pallas_call | solution.py:625
  62.0 1.3 %copy.10 = bf16[512,2048]{1,0:T(8,128)(2,1)} copy(bf16[512,2048]{1,0:T(8,128)(2,1)S(1)} %shard_map.82) | data formatting | bytes 4194304

commit v3 on v2

--- a/solution.py
+++ b/solution.py
@@ -14,9 +14,10 @@
 SIZES = (2, 2, 2, 2)
 PLAIN = 1
 SUB = 8
-VIA_Z = (0,)
-VIA_Y = (1, 2, 3, 4, 5)
-STRAIGHT = (6, 7)
+FAR_Z = (0,)
+FAR_X = (6, 7)
+NEAR_Z = (0, 1, 2, 3)
+NEAR_X = ()
 F32 = jnp.float32
 BF16 = jnp.bfloat16
 
@@ -120,26 +121,24 @@
     place_z = place + 2 - 4 * bit_z
 
     def wx(j):
-        return to(ow_hbm.at[strip(place, j)], wo.at[side, strip(place, j)], wxs.at[j], wxr.at[j], across)
+        return to(ow_hbm.at[strip(place, j)], wo.at[side, strip(place, j)], wxs.at[0], wxr.at[j], across)
 
     def wy(j):
         at = strip(place, j)
-        return on_seq(far_wo.at[at], far_wo.at[at], wys.at[j], wyr.at[j], next_y)
+        return on_seq(far_wo.at[at], far_wo.at[at], wys.at[0], wyr.at[j], next_y)
 
     def wz(j):
         at = strip(place, j)
-        return on_seq(far_wo.at[at], far_wo.at[at], wzs.at[j], wzr.at[j], next_z)
+        return on_seq(far_wo.at[at], far_wo.at[at], wzs.at[0], wzr.at[j], next_z)
 
     def wc(j):
         at = strip(3 - place, j)
-        return to(ow_hbm.at[at], wo.at[side, at], wcs.at[j], wcr.at[j], across)
-
-    def corner(j):
-        if j in VIA_Z:
-            at = strip(place_y, j)
-            return on_seq(far_wo.at[at], far_wo.at[at], wcs.at[j], wcr.at[j], next_z)
-        at = strip(place_z, j)
-        return on_seq(far_wo.at[at], far_wo.at[at], wcs.at[j], wcr.at[j], next_y)
+        return to(ow_hbm.at[at], wo.at[side, at], wcs.at[0], wcr.at[j], across)
+
+    def corner(j, over_z):
+        owner, other = (place_y, next_z) if over_z else (place_z, next_y)
+        at = strip(owner, j)
+        return on_seq(far_wo.at[at], far_wo.at[at], wcs.at[0], wcr.at[j], other)
 
     far_half = me >= blocks // 2
 
@@ -156,12 +155,40 @@
 
     near = jnp.logical_not(far_half)
 
-    def pass_corner(j):
-        if j in VIA_Z:
-            wy(j).wait_recv()
-        else:
-            wz(j).wait_recv()
-        corner(j).start()
+    def by_half(body):
+        @pl.when(far_half)
+        def _():
+            body(FAR_Z, FAR_X)
+
+        @pl.when(near)
+        def _():
+            body(NEAR_Z, NEAR_X)
+
+    def pass_corners(over_z, straight):
+        for j in range(SUB):
+            if j in straight:
+                continue
+            if j in over_z:
+                wy(j).wait_recv()
+            else:
+                wz(j).wait_recv()
+            corner(j, j in over_z).start()
+
+    def take_pieces(over_z, straight):
+        for j in range(SUB):
+            if j in straight or j not in over_z:
+                wy(j).wait_recv()
+            if j in straight or j in over_z:
+                wz(j).wait_recv()
+            if j in straight:
+                wc(j).wait_recv()
+            else:
+                corner(j, j in over_z).wait_recv()
+
+    def drain_pieces():
+        sent = far_wo.at[pl.ds(pl.multiple_of(place * quarter, quarter), quarter)]
+        for sem in (wxs, wys, wzs, wcs):
+            to(sent, sent, sem.at[0], wxr.at[0], across).wait_send()
 
     runs = rows // 128
     tri = (
@@ -187,14 +214,16 @@
         carried = run[:, 127:128]
     loads[0].start()
 
-    def enter():
+    def enter(straight):
         pl.semaphore_wait(barrier, greeted)
         for j in range(SUB):
             wx(j).start()
-        for j in STRAIGHT:
+        for j in straight:
             wc(j).start()
 
-    pl.when(me >= blocks // 2)(enter)
+    @pl.when(far_half)
+    def _():
+        enter(FAR_X)
 
     def norm_chunk(r, carry):
         at = pl.ds(pl.multiple_of(r * chunk, chunk), chunk)
@@ -223,7 +252,11 @@
     for c in range(2):
         cols = slice(c * (inner // 2), (c + 1) * (inner // 2))
         k[:, cols] = dot(normed[...], wk[:, cols]).astype(BF16)
-    pl.when(near)(enter)
+
+    @pl.when(near)
+    def _():
+        enter(NEAR_X)
+
     loads[1].wait()
 
     low = lax.broadcasted_iota(jnp.int32, (1, 128), 1) < 64
@@ -352,6 +385,8 @@
                 weights = (scores * 0.125 * jnp.exp(gaps)).astype(BF16)
                 sums.append(dot(weights, v[:reach, lanes]))
             att[at, lanes] = jnp.where(low, sums[0], sums[1])
+            if p == 0 and piece:
+                pass_pieces(near, (("wy", 0), ("wy", 1)))
             if p % 2 == 0 and piece and taken < steps:
                 take_state(taken)
                 taken += 1
@@ -359,12 +394,13 @@
                     pass_pieces(far_half, (("y", 0), ("y", 1), ("wy", 2)))
                 elif taken == 2:
                     pass_pieces(far_half, (("wy", 4),))
-                    pass_pieces(near, (("wyz", 0),))
+                    pass_pieces(near, (("z", 0), ("z", 1), ("z", 2), ("wyz", 3)))
         if p == 1:
             pass_pieces(far_half, (("wy", 3),))
+            pass_pieces(near, (("wy", 2),))
         if p == pairs - 1:
             pass_pieces(far_half, (("wy", 5),))
-            pass_pieces(near, (("wyz", 1),))
+            pass_pieces(near, (("wyz", 4),))
     while taken < steps:
         take_state(taken)
         taken += 1
@@ -406,31 +442,31 @@
 
     def d1(r):
         at = half_rows(r)
-        return to(dsend1.at[at], drecv1.at[at], d1s.at[r], d1r.at[r], partner)
+        return to(dsend1.at[at], drecv1.at[at], d1s.at[0], d1r.at[r], partner)
 
     def x1(r):
         at = half_rows(r)
-        return to(xsend1.at[at], xrecv1.at[at], x1s.at[r], x1r.at[r], across)
+        return to(xsend1.at[at], xrecv1.at[at], x1s.at[0], x1r.at[r], across)
 
     def hx(r):
         at = whole_rows(r)
-        return to(ho.at[side, at], ho.at[side, at], hs.at[r], hr.at[r], across)
+        return to(ho.at[side, at], ho.at[side, at], hs.at[0], hr.at[r], across)
 
     def nfc(r):
-        return to(nf.at[own_rows(r)], nf.at[own_rows(r)], ns.at[r], nr.at[r], partner)
+        return to(nf.at[own_rows(r)], nf.at[own_rows(r)], ns.at[0], nr.at[r], partner)
 
     def d2(r):
         at = half_rows(r)
-        return to(dsend2.at[at], drecv2.at[at], d2s.at[r], d2r.at[r], partner)
+        return to(dsend2.at[at], drecv2.at[at], d2s.at[0], d2r.at[r], partner)
 
     def x2(r, piece):
         n = sizes[r] // 4
         at = pl.ds(starts[r] // 2 + piece * n, n)
-        return to(xsend2.at[at], xrecv2.at[at], x2s.at[r, piece], x2r.at[r, piece], across)
+        return to(xsend2.at[at], xrecv2.at[at], x2s.at[0], x2r.at[r, piece], across)
 
     def oc(r, piece):
         at = out_rows(r, piece)
-        return to(out.at[at], out.at[at], osd.at[r, piece], orv.at[r, piece], partner)
+        return to(out.at[at], out.at[at], osd.at[0], orv.at[0], partner)
 
     def out_rows(r, piece):
         n = sizes[r] // 4
@@ -521,27 +557,19 @@
         attend(r)
         combine(r)
     pass_pieces(far_half, (("wyz", 7),))
-    pass_pieces(near, (("wyz", 2), ("wyz", 3)))
+    pass_pieces(near, (("wyz", 5),))
     for r in range(PLAIN + 1, count):
         attend(r)
     for r in range(PLAIN):
         cross(r)
     for r in range(PLAIN + 1, count):
         hx(r).start()
-    pass_pieces(near, [("wyz", j) for j in range(4, SUB)])
+    pass_pieces(near, [("wyz", j) for j in range(6, SUB)])
     for at in (4, 5, 6):
         loads[at].wait()
 
     def arrive():
-        for j in range(SUB):
-            if j not in VIA_Z:
-                wy(j).wait_recv()
-            if j not in VIA_Y:
-                wz(j).wait_recv()
-            if j in STRAIGHT:
-                wc(j).wait_recv()
-            else:
-                corner(j).wait_recv()
+        by_half(take_pieces)
 
     def combine_late(r):
         if r == PLAIN:
@@ -549,8 +577,7 @@
         hx(r).wait_recv()
         combine(r)
 
-    for j in VIA_Z + VIA_Y:
-        pass_corner(j)
+    by_half(pass_corners)
     settle(0)
     for r in range(count):
         if PLAIN < r + 1 < count:
@@ -565,24 +592,25 @@
         if r + 1 < count:
             settle(r + 1)
     pass_sums(count - 1)
-    for j in range(SUB):
-        for copy in (wx(j), wy(j), wz(j), wc(j) if j in STRAIGHT else corner(j)):
-            copy.wait_send()
+    drain_pieces()
     for step in range(steps):
         @pl.when(sends(step))
         def _():
             for copy in state_copies(step):
                 copy.wait_send()
-    for r in range(count):
-        for copy in (d1(r), nfc(r), d2(r), x1(r) if r < PLAIN else hx(r)):
-            copy.wait_send()
+    to(dsend1, dsend1, d1s.at[0], d1r.at[0], partner).wait_send()
+    to(dsend1, dsend1, ns.at[0], nr.at[0], partner).wait_send()
+    to(dsend2, dsend2, d2s.at[0], d2r.at[0], partner).wait_send()
+    if PLAIN:
+        to(xsend1, xsend1, x1s.at[0], x1r.at[0], across).wait_send()
+    if PLAIN < count:
+        late = ho.at[side, slice(starts[PLAIN], rows)]
+        to(late, late, hs.at[0], hr.at[PLAIN], across).wait_send()
     for r in range(count):
         for piece in range(2):
             finish(r, piece)
-    for r in range(count):
-        for piece in range(2):
-            x2(r, piece).wait_send()
-            oc(r, piece).wait()
+    to(xsend2, xsend2, x2s.at[0], x2r.at[0, 0], across).wait_send()
+    to(xsend2, xrecv2, osd.at[0], orv.at[0], partner).wait()
 
 
 def local(blocks, tokens, forget, attn_gain, projections, out_weight, ffn_gain, expand_weight, down_weight):
@@ -619,7 +647,7 @@
         halves, halves, halves, halves,
         V((inner, rows), BF16), V((rows, heads), F32), V((heads, rows), F32),
         S((8,)), S((CHUNKS,)), S((3,)), S((slots, 3)), S((slots, 3)),
-    ] + [S((SUB,)) for _ in range(8)] + [S((count,)) for _ in range(10)] + [S((count, 2)) for _ in range(4)]
+    ] + [S((1,)), S((SUB,))] * 4 + [S((1,)), S((count,)), S((1,)), S((max(PLAIN, 1),))] + [S((1,)), S((count,))] * 3 + [S((1,)), S((count, 2)), S((1,)), S((1,))]
     hbm = pl.BlockSpec(memory_space=pl.ANY)
     vmem = pl.BlockSpec(memory_space=pltpu.VMEM)
     return pl.pallas_call(

time: 63.4 us -> 62 us (0.978)
  Pallas kernels: 62 us -> 60.5 us
    pallas_call x1, Pallas kernels: 62 us -> 60.5 us  [local(): pl.pallas_call(functools.partial(kernel, blocks, steps), out_shape=pltpu....]
where the time goes in v3:
time: 62 us; the launch traced here: 61.8 us
  Pallas kernels  60.5 us (98%)
  local copies, waits for them, and re-layouts  1.32 us (2%)
    pallas_call x1, Pallas kernels, local(): pl.pallas_call(functools.partial(kernel, blocks, steps), out_shape=pltpu....  60.5 us
    unnamed x1, local copies, waits for them, and re-layouts  1.32 us

profile of v3, /device:TPU:0, one launch (start us, length us, event | category | flops | bytes accessed | tf_op | source)
XLA Modules:
  0.0 61.8 jit_solution(13770562093702733759)
XLA Ops:
  0.0 60.5 %shard_map.82 = bf16[512,2048]{1,0:T(8,128)(2,1)S(1)} custom-call(bf16[512,2048]{1,0:T(8,128)(2,1)} %tok_hbm.1, f32[8,512]{1,0:T(8,128)} %bitcast.3, f32[1,2048]{1,0:T(1,128)} %bitcast.4, bf16[3,2048,512]{2,1,0:T(8,128)(2,1)} %proj_hbm.1, bf16[512,2048]{1,0:T(8,128)(2,1)} %ow_hbm.1, f32[1,2048]{1,0:T(1,128)} %bitcast.5, bf16[2,2048,1024]{2,1,0:T(8,128)(2,1)} %ew_hbm.1, ...), custom_call_target="tpu_custom_call" | custom-call | tf_op jit(solution)/shard_map/pallas_call | solution.py:653
  60.5 1.3 %copy.10 = bf16[512,2048]{1,0:T(8,128)(2,1)} copy(bf16[512,2048]{1,0:T(8,128)(2,1)S(1)} %shard_map.82) | data formatting | bytes 4194304

commit v4 on v3

--- a/solution.py
+++ b/solution.py
@@ -586,8 +586,10 @@
             pass_sums(r - 1)
         forward(r)
         if r + 1 == PLAIN < count:
+            pl.when(near)(functools.partial(pass_sums, r))
             combine_late(r + 1)
-        if r < PLAIN:
+            pl.when(far_half)(functools.partial(pass_sums, r))
+        elif r < PLAIN:
             pass_sums(r)
         if r + 1 < count:
             settle(r + 1)

time: 62 us -> 63.5 us (1.024)
  Pallas kernels: 60.5 us -> 62 us
    pallas_call x1, Pallas kernels: 60.5 us -> 62 us  [local(): pl.pallas_call(functools.partial(kernel, blocks, steps), out_shape=pltpu....]
where the time goes in v4:
time: 63.5 us; the launch traced here: 63.3 us
  Pallas kernels  62 us (98%)
  local copies, waits for them, and re-layouts  1.32 us (2%)
    pallas_call x1, Pallas kernels, local(): pl.pallas_call(functools.partial(kernel, blocks, steps), out_shape=pltpu....  62 us
    unnamed x1, local copies, waits for them, and re-layouts  1.32 us

profile of v4, /device:TPU:0, one launch (start us, length us, event | category | flops | bytes accessed | tf_op | source)
XLA Modules:
  0.0 63.3 jit_solution(18188357330186551868)
XLA Ops:
  0.0 62.0 %shard_map.82 = bf16[512,2048]{1,0:T(8,128)(2,1)S(1)} custom-call(bf16[512,2048]{1,0:T(8,128)(2,1)} %tok_hbm.1, f32[8,512]{1,0:T(8,128)} %bitcast.3, f32[1,2048]{1,0:T(1,128)} %bitcast.4, bf16[3,2048,512]{2,1,0:T(8,128)(2,1)} %proj_hbm.1, bf16[512,2048]{1,0:T(8,128)(2,1)} %ow_hbm.1, f32[1,2048]{1,0:T(1,128)} %bitcast.5, bf16[2,2048,1024]{2,1,0:T(8,128)(2,1)} %ew_hbm.1, ...), custom_call_target="tpu_custom_call" | custom-call | tf_op jit(solution)/shard_map/pallas_call | solution.py:655
  62.0 1.3 %copy.10 = bf16[512,2048]{1,0:T(8,128)(2,1)} copy(bf16[512,2048]{1,0:T(8,128)(2,1)S(1)} %shard_map.82) | data formatting | bytes 4194304
